TPU v7x, 768 devices: a whole 4x8x12 slice. The times are simulated.
768 devices in a mesh: rep: 12 (over z), own: 64 (over y, x, core).
Axes of the slice: x: 4, y: 8, z: 12, core: 2. Of those that a mesh axis runs over, the one named last changes fastest.
Arguments:
- grads: float32 [384, 576, 1024], P('rep', 'own'), may hold values from -60 to 60
- momentum: bfloat16 [768, 576, 1024], P(('rep', 'own')), may hold values from -6 to 6
- owner_table: int32 [12, 64], replicated, may hold values from 0 to 63, each once within a row
Outputs:
- new_momentum: bfloat16 [768, 576, 1024], P(('rep', 'own'))
- updates: bfloat16 [384, 576, 1024], P(None, 'own')
Inputs may be any that keep to these rules, and one draw needn't show every extreme that they name: Each row of owner_table is a permutation of 0 to 63; entries of 32 or more mark empty slots.
All inputs are finite; a program needn't handle non-finite values.
Results may differ from a plain program's by a relative error of at most 0.01.
Values may be sent and summed in bfloat16 or wider, within the bound.
A program may use at most 128 MiB of HBM per device.

v0:
```python
import math

import jax
import jax.numpy as jnp
from jax import lax
from jax.sharding import Mesh
from jax.sharding import PartitionSpec as P

ITERS = 2
OWN = ("own_0", "own_1", "own_2")
REP_OWN = ("rep", "own_0", "own_1", "own_2")


DECAY = 0.95
COEF_A = 3.4445
COEF_B = -4.775
COEF_C = 2.0315
EPSILON = 1e-07


def split_up(array, dim, size):
    before, after = (array.shape[:dim], array.shape[dim + 1 :])
    return jnp.moveaxis(array.reshape(*before, size, -1, *after), dim, 0)


def in_order(parts, dim):
    shape = list(parts.shape[1:])
    shape[dim] *= parts.shape[0]
    return jnp.moveaxis(parts, 0, dim).reshape(shape)


def turned_blocks(parts, axes, sequence):
    inside = parts.shape[1:]
    whole = parts.reshape(*(lax.axis_size(a) for a in axes), *inside)
    for k in sequence:
        whole = lax.all_to_all(whole, axes[k], k, k, tiled=True)
    return whole.reshape(-1, *inside)


def two_step_exchange(array, groups, sequence, split_dim, concat_dim):
    size = lax.axis_size(groups[0]) * lax.axis_size(groups[1])
    parts = split_up(array, split_dim, size)
    return in_order(turned_blocks(parts, groups, sequence), concat_dim)


def orthogonalize(blend):
    total = jnp.sqrt(jnp.sum(blend * blend))
    iterate = (blend / (total + EPSILON)).astype(jnp.bfloat16)
    factor = 0.2 * math.sqrt(max(blend.shape[0], blend.shape[1]))
    result = None
    for turn in range(ITERS):
        gram = jnp.dot(iterate, iterate.T, preferred_element_type=jnp.float32).astype(jnp.bfloat16)
        square = jnp.dot(gram, gram, preferred_element_type=jnp.float32)
        poly = (COEF_B * gram.astype(jnp.float32) + COEF_C * square).astype(jnp.bfloat16)
        mixed = COEF_A * iterate.astype(jnp.float32) + jnp.dot(
            poly, iterate, preferred_element_type=jnp.float32
        )
        if turn + 1 < ITERS:
            iterate = mixed.astype(jnp.bfloat16)
        else:
            result = (factor * mixed).astype(jnp.bfloat16)
    return result


def body(grads, momentum, owner_table):
    group = lax.axis_index("rep")
    slot_matrix = lax.dynamic_index_in_dim(owner_table, group, 0, keepdims=False)
    matrix_count, shard_rows, columns = grads.shape
    is_live = slot_matrix < matrix_count
    clamped = jnp.minimum(slot_matrix, matrix_count - 1)
    half_grads = grads.astype(jnp.bfloat16)
    outgoing = jnp.take(half_grads, clamped, axis=0) * is_live[:, None, None].astype(jnp.bfloat16)
    incoming = lax.all_to_all(outgoing, OWN, split_axis=0, concat_axis=1, tiled=True)
    gradient = incoming[0].astype(jnp.float32)
    moment = DECAY * momentum[0].astype(jnp.float32) + gradient
    new_momentum = moment.astype(jnp.bfloat16)[None]
    update = orthogonalize(gradient + DECAY * moment)
    returned = two_step_exchange(update[None], (("own_0", "own_1"), "own_2"), (1, 0), 1, 0)
    holders = jnp.argsort(slot_matrix)[:matrix_count]
    grouped = jnp.take(returned, holders, axis=0)
    updates = lax.all_gather(grouped, "rep", axis=0, tiled=True)
    return (new_momentum, updates)


def solution(mesh):
    split = Mesh(
        mesh.devices.reshape(mesh.shape["rep"], 8, 4, 2), ("rep", "own_0", "own_1", "own_2")
    )
    placed = (P("rep", OWN, None), P(REP_OWN, None, None), P())
    return jax.shard_map(
        body,
        mesh=split,
        in_specs=placed,
        out_specs=(P(REP_OWN, None, None), P(None, OWN, None)),
        check_vma=False,
    )
```

profile of v0, /device:TPU:1, one launch (start us, length us, event | category | flops | bytes accessed | tf_op | source)
XLA Modules:
  0.0 264.2 jit_solution(17909337350316603338)
XLA Ops:
  7.2 0.7 fusion.9
  7.9 0.7 compare_convert_fusion
  8.6 1.4 convert_element_type.90
  9.9 0.4 copy.15
  10.3 0.7 gather_fusion
  11.0 0.3 select_multiply_fusion
  11.3 63.7 %all_to_all.19 = bf16[64,9,1024]{2,1,0:T(8,128)(2,1)S(1)} all-to-all(bf16[64,9,1024]{2,1,0:T(8,128)(2,1)S(1)} %select_multiply_fusion), channel_id=1, replica_groups=mesh['rep'=12,'own_0'=8,'own_1'=4,'own_2'=2] {'own_0','own_1','own_2'}, dimensions={0} | all-to-all | bytes 2359296 | tf_op jit(solution)/shard_map/all_to_all | solution.py:73
  75.0 0.0 copy-start
  75.0 1.6 reshape.85
  76.7 0.0 copy-done
  76.7 4.1 %convert_multiply_fusion = (f32[1,576,1024]{2,1,0:T(8,128)}, bf16[1,576,1024]{2,1,0:T(8,128)(2,1)}) fusion(bf16[1,576,1024]{2,1,0:T(8,128)(2,1)S(1)} %copy-done, f32[1,576,1024]{2,1,0:T(8,128)} %reshape.85), kind=kLoop, calls=%fused_computation.12 | loop fusion | flops 2359296 | bytes 7077888 | tf_op jit(solution)/shard_map/mul | solution.py:75
  80.8 3.9 %mul.65 = f32[64,9,1024]{2,1,0:T(8,128)} reshape(f32[1,576,1024]{2,1,0:T(8,128)} %get-tuple-element.10) | data formatting | bytes 4718592 | tf_op jit(solution)/shard_map/mul | solution.py:75
  84.7 4.0 %multiply_reduce_fusion = f32[]{:T(128)} fusion(f32[64,9,1024]{2,1,0:T(8,128)} %mul.65, bf16[64,9,1024]{2,1,0:T(8,128)(2,1)S(1)} %all_to_all.19), kind=kLoop, calls=%fused_computation.3 | loop fusion | flops 3538943 | bytes 3538948 | tf_op jit(solution)/shard_map/reduce_sum | solution.py:47
  89.4 4.4 %divide_convert_fusion = bf16[64,9,1024]{2,1,0:T(8,128)(2,1)} fusion(f32[]{:T(128)S(6)} %add.81, f32[64,9,1024]{2,1,0:T(8,128)} %mul.65, bf16[64,9,1024]{2,1,0:T(8,128)(2,1)S(1)} %all_to_all.19), kind=kLoop, calls=%fused_computation.2 | loop fusion | flops 3538944 | bytes 4718596 | tf_op jit(solution)/shard_map/convert_element_type | solution.py:48
  93.8 3.6 %convert_element_type.101 = bf16[576,1024]{1,0:T(8,128)(2,1)} reshape(bf16[64,9,1024]{2,1,0:T(8,128)(2,1)} %divide_convert_fusion) | data formatting | bytes 2359296 | tf_op jit(solution)/shard_map/convert_element_type | solution.py:48
  97.4 3.7 %convolution_convert_fusion.1 = bf16[576,576]{1,0:T(8,128)(2,1)} fusion(bf16[576,1024]{1,0:T(8,128)(2,1)} %convert_element_type.101), kind=kOutput, calls=%fused_computation.18 | convolution fusion | flops 679809024 | bytes 1843200 | tf_op jit(solution)/shard_map/dot_general | solution.py:52
  101.1 1.6 reshape.86
  102.7 5.1 %add_convert_fusion = bf16[576,1024]{1,0:T(8,128)(2,1)S(1)} fusion(f32[]{:T(128)S(6)} %add.81, f32[576,1024]{1,0:T(8,128)} %reshape.86, bf16[576,576]{1,0:T(8,128)(2,1)} %convolution_convert_fusion.1, bf16[1,576,1024]{2,1,0:T(8,128)(2,1)S(1)} %copy-done), kind=kOutput, calls=%fused_computation.10 | convolution fusion | flops 1073958912 | bytes 5382148 | tf_op jit(solution)/shard_map/dot_general | solution.py:55
  107.8 1.1 convolution_convert_fusion
  109.0 1.7 multiply_convert_fusion
  110.7 0.5 reshape_transpose_reshape_broadcast_in_dim.3
  111.2 0.7 copy.16
  111.9 6.3 %all_to_all.20 = bf16[32,2,1,9,1024]{4,0,3,2,1:T(8,128)(2,1)S(1)} all-to-all(bf16[32,2,1,9,1024]{4,0,3,2,1:T(8,128)(2,1)S(1)} %copy.16), channel_id=1, replica_groups=mesh['rep'=12,'own_0'=8,'own_1'=4,'own_2'=2] {'own_2'}, dimensions={1} | all-to-all | bytes 2359296 | tf_op jit(solution)/shard_map/all_to_all | solution.py:36
  118.2 2.2 copy.17
  120.4 4.4 %all-to-all-start.2 = ((bf16[32,2,1,9,1024]{4,1,3,2,0:T(2,128)(2,1)}), bf16[32,2,1,9,1024]{4,1,3,2,0:T(2,128)(2,1)S(1)}, u32[]{:S(2)}, u32[]{:S(2)}) async-start(bf16[32,2,1,9,1024]{4,1,3,2,0:T(2,128)(2,1)} %copy.17), calls=%async_computation.2 | async-start | bytes 2359296 | tf_op jit(solution)/shard_map/all_to_all | solution.py:36
  124.9 0.0 all-gather.2.cloned.1.call-start
  124.9 2.1 sort.17
  127.1 27.4 %all-to-all-done.2 = bf16[32,2,1,9,1024]{4,1,3,2,0:T(2,128)(2,1)S(1)} async-done(((bf16[32,2,1,9,1024]{4,1,3,2,0:T(2,128)(2,1)}), bf16[32,2,1,9,1024]{4,1,3,2,0:T(2,128)(2,1)S(1)}, u32[]{:S(2)}, u32[]{:S(2)}) %all-to-all-start.2) | async-done | bytes 1179680 | tf_op jit(solution)/shard_map/all_to_all | solution.py:36
  154.5 0.5 copy.18
  155.0 0.6 gather_fusion.1
  155.6 0.2 broadcast_select_fusion
  155.8 1.2 copy.19
  157.0 0.0 all-gather.2.cloned.1.call-update
  157.0 93.6 %all-gather.2.cloned.1.call-done = bf16[384,9,1024]{2,0,1:T(8,128)(2,1)} async-done(((bf16[32,9,1024]{2,0,1:T(8,128)(2,1)}), bf16[384,9,1024]{2,0,1:T(8,128)(2,1)}) %all-gather.2.cloned.1.call-update) | async-done | bytes 7077904 | tf_op jit(solution)/shard_map/all_gather | solution.py:81
  250.6 6.8 %copy.21 = bf16[384,9,1024]{2,0,1:T(8,128)(2,1)} copy(bf16[384,9,1024]{2,0,1:T(8,128)(2,1)} %all-gather.2.cloned.1.call-done) | data formatting | bytes 14155776
  (5 shorter events, 0.0 us)
Async XLA Ops:
  75.0 1.6 copy-start
  120.4 34.0 %all-to-all-start.2 = ((bf16[32,2,1,9,1024]{4,1,3,2,0:T(2,128)(2,1)}), bf16[32,2,1,9,1024]{4,1,3,2,0:T(2,128)(2,1)S(1)}, u32[]{:S(2)}, u32[]{:S(2)}) async-start(bf16[32,2,1,9,1024]{4,1,3,2,0:T(2,128)(2,1)} %copy.17), calls=%async_computation.2 | async-start | bytes 2359296 | tf_op jit(solution)/shard_map/all_to_all | solution.py:36
  124.9 125.7 %all-gather.2.cloned.1.call-start = ((), (), s32[]{:S(2)}) async-start(), calls=%async_computation.3 | async-start | bytes 7667712 | tf_op jit(solution)/shard_map/all_gather | solution.py:81
Sparse Core Ops, SparseCore 0:
  157.1 93.4 all-gather.1
where the time goes:
time: 265 us; the launch traced here: 264 us
  waiting for transfers between devices  121 us (46%)
  blocking collectives  70 us (26%)
  local copies, waits for them, and re-layouts  24.4 us (9%)
  other arithmetic  17.8 us (7%)
  between operations  14.9 us (6%)
  matrix products  11.7 us (4%)
  starting transfers between devices  4.48 us (2%)
    all_gather x1, waiting for transfers between devices, body(): updates = lax.all_gather(grouped, 'rep', axis=0, tiled=True)  93.6 us
    all_to_all x1, blocking collectives, body(): lax.all_to_all(outgoing, OWN, split_axis=0, concat_axis=1, tiled=True)  63.7 us
    all_to_all x1, waiting for transfers between devices, turned_blocks(): whole = lax.all_to_all(whole, axes[k], k, k, tiled=True)  27.4 us
    dot_general x2, matrix products, orthogonalize(): jnp.dot(poly, iterate, preferred_element_type=jnp.float32)  6.88 us
    unnamed x3, local copies, waits for them, and re-layouts  6.78 us
    all_to_all x1, blocking collectives, turned_blocks(): whole = lax.all_to_all(whole, axes[k], k, k, tiled=True)  6.27 us
  transfers between devices with their start and end apart: 2, of which 2 were waited for; matrix products, arithmetic and copies ran while one was open for 1% of the time, Pallas kernels for 0%

commit v1 on v0

v1 whole, which is shorter than its diff:
```python
import functools
import math

import jax
import jax.numpy as jnp
from jax import lax
from jax.experimental import pallas as pl
from jax.experimental.pallas import tpu as pltpu
from jax.sharding import PartitionSpec as P

ITERS = 2
DECAY = 0.95
COEF_A = 3.4445
COEF_B = -4.775
COEF_C = 2.0315
EPSILON = 1e-07
LANES = 128
MESH = pl.DeviceIdType.MESH

CHUNKS = (1, 2, 3, 3)
ORDER = (
    (0, 0), (0, 1), (1, 0), (0, 2), (1, 1), (0, 3), (1, 2), (0, 4),
    (2, 0), (1, 3), (0, 5), (2, 1), (1, 4), (3, 0), (2, 2), (1, 5),
    (3, 1), (2, 3), (3, 2), (2, 4), (3, 3), (2, 5), (3, 4), (3, 5),
)


def kernel(
    n_rep, n_own, mats,
    grads, momentum, table, new_momentum, updates,
    outgoing, incoming, blend, iterate, iterate2, gram, poly, rows_out,
    back0, back1, back2, back3, tile_a, tile_b, tile_c,
    send_in, recv_in, send_back, recv_back, send_ring, recv_ring,
):
    z, me = lax.axis_index("rep"), lax.axis_index("own")
    shard, _, cols = grads.shape
    rows = shard * n_own
    pieces = cols // LANES
    back = (back0, back1, back2, back3)
    up, down = lax.rem(z + 1, n_rep), lax.rem(z + n_rep - 1, n_rep)

    barrier = pltpu.get_barrier_semaphore()

    def greet(i, _):
        peer = lax.rem(me + i, n_own)
        pl.semaphore_signal(barrier, inc=1, device_id=(z, peer), device_id_type=MESH)
        return 0

    lax.fori_loop(1, n_own, greet, 0)
    for other in (up, down):
        pl.semaphore_signal(barrier, inc=1, device_id=(other, me), device_id_type=MESH)

    slots = jnp.broadcast_to(table[pl.ds(z, 1), :], (mats, n_own))
    matrices = lax.broadcasted_iota(jnp.int32, (mats, n_own), 0)
    holds = (slots == matrices).astype(jnp.float32)
    picks = holds.astype(jnp.bfloat16)
    spreads = holds.T.astype(jnp.bfloat16)

    def pack(j, _):
        for c in range(pieces):
            tile_a[pl.ds(c, n_own, stride=pieces), :] = jnp.dot(
                spreads,
                grads[j, :, c * LANES : (c + 1) * LANES].astype(jnp.bfloat16),
                preferred_element_type=jnp.float32,
            )
        outgoing[:, j] = tile_a[...].reshape(n_own, pieces, LANES).astype(jnp.bfloat16)
        return 0

    lax.fori_loop(0, shard, pack, 0)
    for j in range(shard):
        incoming[me * shard + j] = outgoing[me, j]
    pl.semaphore_wait(barrier, n_own + 1)

    def give(i, _):
        peer = lax.rem(me + i, n_own)
        pltpu.make_async_remote_copy(
            src_ref=outgoing.at[peer],
            dst_ref=incoming.at[pl.ds(me * shard, shard)],
            send_sem=send_in, recv_sem=recv_in, device_id=(z, peer), device_id_type=MESH,
        ).start()
        return 0

    lax.fori_loop(1, n_own, give, 0)
    pltpu.make_async_copy(
        incoming.at[pl.ds(0, (n_own - 1) * shard)], incoming.at[pl.ds(0, (n_own - 1) * shard)], recv_in
    ).wait()

    block = 16

    def combine(i, total):
        at = pl.multiple_of(i * block, block)
        tile_b[...] = incoming[pl.ds(at, block)].astype(jnp.float32).reshape(block * pieces, LANES)
        for c in range(pieces):
            here = (pl.ds(at, block), pl.ds(c * LANES, LANES))
            gradient = tile_b[pl.ds(c, block, stride=pieces), :]
            moment = DECAY * momentum[here].astype(jnp.float32) + gradient
            new_momentum[here] = moment.astype(jnp.bfloat16)
            mixed = gradient + DECAY * moment
            blend[here] = mixed
            total = total + mixed * mixed
        return total

    total = lax.fori_loop(0, rows // block, combine, jnp.zeros((block, LANES), jnp.float32))
    norm = jnp.sqrt(jnp.sum(total, keepdims=True))
    scale = 1.0 / (norm + EPSILON)

    def start(i, _):
        at = pl.ds(pl.multiple_of(i * block, block), block)
        iterate[at, :] = (blend[at, :] * scale).astype(jnp.bfloat16)
        return 0

    lax.fori_loop(0, rows // block, start, 0)

    band = rows // 3
    factor = 0.2 * math.sqrt(max(rows, cols))
    for turn in range(ITERS):
        now, later = (iterate, iterate2) if turn % 2 == 0 else (iterate2, iterate)

        def gram_band(i, _):
            at = pl.ds(pl.multiple_of(i * band, band), band)
            gram[at, :] = lax.dot_general(
                now[at, :], now[...], (((1,), (1,)), ((), ())), preferred_element_type=jnp.float32
            ).astype(jnp.bfloat16)
            return 0

        lax.fori_loop(0, 3, gram_band, 0)

        def poly_band(i, _):
            at = pl.ds(pl.multiple_of(i * band, band), band)
            mine = gram[at, :]
            square = jnp.dot(mine, gram[...], preferred_element_type=jnp.float32)
            poly[at, :] = (COEF_B * mine.astype(jnp.float32) + COEF_C * square).astype(jnp.bfloat16)
            return 0

        lax.fori_loop(0, 3, poly_band, 0)

        def mixed_band(i, _):
            at = pl.ds(pl.multiple_of(i * band, band), band)
            for wide in range(0, cols, 256):
                mixed = COEF_A * now[at, wide : wide + 256].astype(jnp.float32) + jnp.dot(
                    poly[at, :], now[:, wide : wide + 256], preferred_element_type=jnp.float32
                )
                if turn + 1 < ITERS:
                    later[at, wide : wide + 256] = mixed.astype(jnp.bfloat16)
                else:
                    mixed = factor * mixed
                    for c in range(2):
                        tile_c[pl.ds(wide // LANES + c, band, stride=pieces), :] = mixed[
                            :, c * LANES : (c + 1) * LANES
                        ]
            if turn + 1 == ITERS:

                def to_tiles(t, _):
                    piece = tile_c[pl.ds(pl.multiple_of(t * 8 * pieces, 8 * pieces), 8 * pieces), :]
                    rows_out[pl.ds(i * band + t * 8, 8)] = piece.reshape(8, pieces, LANES).astype(jnp.bfloat16)
                    return 0

                lax.fori_loop(0, band // 8, to_tiles, 0)
            return 0

        lax.fori_loop(0, 3, mixed_band, 0)

    first = 0
    firsts = []
    for q, count in enumerate(CHUNKS):
        firsts.append(first)
        back[q][me] = rows_out[pl.ds(me * shard + first, count)]

        def give_back(i, _):
            peer = lax.rem(me + i, n_own)
            pltpu.make_async_remote_copy(
                src_ref=rows_out.at[pl.ds(peer * shard + first, count)],
                dst_ref=back[q].at[me],
                send_sem=send_back.at[q], recv_sem=recv_back.at[q],
                device_id=(z, peer), device_id_type=MESH,
            ).start()
            return 0

        lax.fori_loop(1, n_own, give_back, 0)
        first += count

    half = mats // 2
    last = n_rep // 2 - 1

    def ring(q, step, way):
        source = lax.rem(z + n_rep - step, n_rep) if way == 0 else lax.rem(z + step, n_rep)
        at, count = source * mats, mats
        if step == last:
            at, count = at + way * half, half
        where = updates.at[
            pl.ds(firsts[q], CHUNKS[q]), pl.ds(pl.multiple_of(at, half), count), :
        ]
        return pltpu.make_async_remote_copy(
            src_ref=where, dst_ref=where,
            send_sem=send_ring.at[q, step, way], recv_sem=recv_ring.at[q, step, way],
            device_id=(up if way == 0 else down, me), device_id_type=MESH,
        )

    def arrival(q, step, way):
        source = lax.rem(z + 2 * n_rep - step - 1, n_rep) if way == 0 else lax.rem(z + step + 1, n_rep)
        at, count = source * mats, mats
        if step == last:
            at, count = at + way * half, half
        where = updates.at[
            pl.ds(firsts[q], CHUNKS[q]), pl.ds(pl.multiple_of(at, half), count), :
        ]
        return pltpu.make_async_copy(where, where, recv_ring.at[q, step, way])

    for q, step in ORDER:
        if step == 0:
            got = back[q].at[pl.ds(0, n_own - 1)]
            pltpu.make_async_copy(got, got, recv_back.at[q]).wait()
            for j in range(CHUNKS[q]):

                tile_a[...] = back[q][:, j].astype(jnp.float32).reshape(n_own * pieces, LANES)
                for c in range(pieces):
                    updates[
                        firsts[q] + j, pl.ds(pl.multiple_of(z * mats, mats), mats), c * LANES : (c + 1) * LANES
                    ] = jnp.dot(
                        picks,
                        tile_a[pl.ds(c, n_own, stride=pieces), :].astype(jnp.bfloat16),
                        preferred_element_type=jnp.float32,
                    ).astype(jnp.bfloat16)
        for way in range(2):
            if step > 0:
                arrival(q, step - 1, way).wait()
            ring(q, step, way).start()
    for q in range(len(CHUNKS)):
        for way in range(2):
            arrival(q, last, way).wait()

    pltpu.make_async_copy(
        outgoing.at[pl.ds(0, n_own - 1)], outgoing.at[pl.ds(0, n_own - 1)], send_in
    ).wait()
    for q in range(len(CHUNKS)):
        sent = back[q].at[pl.ds(0, n_own - 1)]
        pltpu.make_async_copy(sent, sent, send_back.at[q]).wait()
        for step in range(last + 1):
            for way in range(2):
                ring(q, step, way).wait_send()


def body(grads, momentum, owner_table):
    n_rep, n_own = lax.axis_size("rep"), lax.axis_size("own")
    mats, shard, cols = grads.shape
    rows = shard * n_own
    pieces = cols // LANES
    vmem = pl.BlockSpec(memory_space=pltpu.VMEM)
    tile = (pieces, LANES)
    chunks = len(CHUNKS)
    new_momentum, updates = pl.pallas_call(
        functools.partial(kernel, n_rep, n_own, mats),
        out_shape=(
            jax.ShapeDtypeStruct((rows, cols), jnp.bfloat16),
            jax.ShapeDtypeStruct((shard, n_rep * mats, cols), jnp.bfloat16),
        ),
        in_specs=[vmem, vmem, vmem],
        out_specs=(vmem, vmem),
        scratch_shapes=[
            pltpu.VMEM((n_own, shard, *tile), jnp.bfloat16),
            pltpu.VMEM((rows, *tile), jnp.bfloat16),
            pltpu.VMEM((rows, cols), jnp.float32),
            pltpu.VMEM((rows, cols), jnp.bfloat16),
            pltpu.VMEM((rows, cols), jnp.bfloat16),
            pltpu.VMEM((rows, rows), jnp.bfloat16),
            pltpu.VMEM((rows, rows), jnp.bfloat16),
            pltpu.VMEM((rows, *tile), jnp.bfloat16),
            *(pltpu.VMEM((n_own, count, *tile), jnp.bfloat16) for count in CHUNKS),
            pltpu.VMEM((n_own * pieces, LANES), jnp.float32),
            pltpu.VMEM((16 * pieces, LANES), jnp.float32),
            pltpu.VMEM((rows // 3 * pieces, LANES), jnp.float32),
            pltpu.SemaphoreType.DMA,
            pltpu.SemaphoreType.DMA,
            pltpu.SemaphoreType.DMA((chunks,)),
            pltpu.SemaphoreType.DMA((chunks,)),
            pltpu.SemaphoreType.DMA((chunks, n_rep // 2, 2)),
            pltpu.SemaphoreType.DMA((chunks, n_rep // 2, 2)),
        ],
        compiler_params=pltpu.CompilerParams(
            collective_id=0, has_side_effects=True, vmem_limit_bytes=40 * 1024 * 1024
        ),
    )(jnp.transpose(grads, (1, 0, 2)), momentum[0], owner_table)
    return (new_momentum[None], jnp.transpose(updates, (1, 0, 2)))


def solution(mesh):
    return jax.shard_map(
        body,
        mesh=mesh,
        in_specs=(P("rep", "own", None), P(("rep", "own"), None, None), P()),
        out_specs=(P(("rep", "own"), None, None), P(None, "own", None)),
        check_vma=False,
    )
```

time: 265 us -> 154 us (0.58)
  Pallas kernels: 0 us -> 144 us
  waiting for transfers between devices: 121 us -> 0 us
  blocking collectives: 70 us -> 0 us
  other arithmetic: 17.8 us -> 0 us
  local copies, waits for them, and re-layouts: 24.4 us -> 7.21 us
  between operations: 14.9 us -> 0.65 us
  matrix products: 11.7 us -> 0 us
  starting transfers between devices: 4.48 us -> 0 us
    pallas_call x0 -> x1, Pallas kernels: none -> 144 us  [body(): pl.pallas_call(functools.partial(kernel, n_rep, n_own, mats), out_shape=(...]
    all_gather x1 -> x0, waiting for transfers between devices: 93.6 us -> none  [body(): updates = lax.all_gather(grouped, 'rep', axis=0, tiled=True)]
    all_to_all x2 -> x0, blocking collectives: 70 us -> none  [the longest x1 63.7 us: body(): lax.all_to_all(outgoing, OWN, split_axis=0, concat_axis=1, tiled=True)]
    all_to_all x1 -> x0, waiting for transfers between devices: 27.4 us -> none  [turned_blocks(): whole = lax.all_to_all(whole, axes[k], k, k, tiled=True)]
    dot_general x4 -> x0, matrix products: 11.7 us -> none  [the longest x2 6.88 us: orthogonalize(): jnp.dot(poly, iterate, preferred_element_type=jnp.float32)]
    convert_element_type x4 -> x0, local copies, waits for them, and re-layouts: 7.19 us -> none  [the longest x1 3.57 us: orthogonalize(): iterate = (blend / (total + EPSILON)).astype(jnp.bfloat16)]
    convert_element_type x3 -> x0, other arithmetic: 6.46 us -> none  [the longest x1 4.41 us: orthogonalize(): iterate = (blend / (total + EPSILON)).astype(jnp.bfloat16)]
    all_to_all x1 -> x0, starting transfers between devices: 4.43 us -> none  [turned_blocks(): whole = lax.all_to_all(whole, axes[k], k, k, tiled=True)]
  transfers between devices with their start and end apart: 2 -> 0, of which waited for: 2 -> 0; matrix products, arithmetic and copies ran while one was open for 1% -> 0% of each run, Pallas kernels for 0% -> 0%
where the time goes in v1:
time: 154 us; the launch traced here: 151 us
  Pallas kernels  144 us (94%)
  local copies, waits for them, and re-layouts  7.21 us (5%)
    pallas_call x1, Pallas kernels, body(): pl.pallas_call(functools.partial(kernel, n_rep, n_own, mats), out_shape=(...  144 us
    unnamed x8, local copies, waits for them, and re-layouts  7.21 us

profile of v1, /device:TPU:1, one launch (start us, length us, event | category | flops | bytes accessed | tf_op | source)
XLA Modules:
  0.0 151.5 jit_solution(6373473719971139903)
XLA Ops:
  0.6 0.0 copy-start
  0.6 1.3 copy-done
  1.9 0.0 copy-start.1
  1.9 1.3 copy-done.1
  3.2 0.0 copy-start.2
  3.2 0.7 copy-done.2
  3.9 143.6 %shard_map.50 = (bf16[576,1024]{1,0:T(8,128)(2,1)S(1)}, bf16[9,384,1024]{2,1,0:T(8,128)(2,1)S(1)}) custom-call(f32[9,32,1024]{2,1,0:T(8,128)S(1)} %bitcast.5, bf16[576,1024]{1,0:T(8,128)(2,1)S(1)} %bitcast.6, s32[12,64]{1,0:T(8,128)S(1)} %copy-done.2), custom_call_target="tpu_custom_call" | custom-call | tf_op jit(solution)/shard_map/pallas_call | solution.py:251
  147.5 1.0 copy.7
  148.5 3.0 %copy.8 = bf16[384,9,1024]{2,0,1:T(8,128)(2,1)} copy(bf16[384,9,1024]{2,0,1:T(8,128)(2,1)S(1)} %bitcast.4) | data formatting | bytes 14155776
Async XLA Ops:
  0.6 1.3 copy-start
  1.9 1.3 copy-start.1
  3.2 0.7 copy-start.2
